TPU v7x, 32 devices: a whole 2x2x4 slice. The times are simulated.
32 devices in a mesh: dp: 4 (over z), tp: 8 (over y, x, core).
Axes of the slice: x: 2, y: 2, z: 4, core: 2. Of those that a mesh axis runs over, the one named last changes fastest.
Arguments:
- ids: int32 [32, 256], P('dp'), parts along dimension 0
- E: bfloat16 [16384, 3072], P('tp')
- g: bfloat16 [3072], replicated
- W: bfloat16 [3072, 5120], P(None, 'tp')
- du: bfloat16 [32, 256, 5120], P('dp', None, 'tp'), parts along dimension 0
- dres: bfloat16 [32, 256, 3072], P('dp', 'tp'), parts along dimension 0
Outputs:
- output 1: bfloat16 [32, 256, 5120], P('dp', None, 'tp'), parts along dimension 0
- output 2: bfloat16 [32, 256, 3072], P('dp', 'tp'), parts along dimension 0
- output 3: float32 [65536, 3072], P(('dp', 'tp')), parts along dimension 0
- output 4: float32 [12288, 5120], P('dp', 'tp'), parts along dimension 0
- output 5: float32 [12288], P('dp'), parts along dimension 0
There are 4 independent parts. A program takes and returns all parts, laid end to end along the dimension named above; an argument that names none is the same for every part.
All inputs are finite; a program needn't handle non-finite values.
Results may differ from a plain program's by a relative error of at most 0.00687744.
Values are sent between devices in bfloat16 or wider.
A program may use at most 1 GiB of HBM per device.

v0:
```python
import jax
import jax.numpy as jnp
from jax import lax
from jax.sharding import PartitionSpec as P

EPS = 1e-6


def solution(mesh):
    ntp = mesh.shape["tp"]

    def body(ids, E, g, W, du, dres):
        vs, d = E.shape
        nk, t = ids.shape
        ts = t // ntp
        me = lax.axis_index("tp")
        lo = me * vs
        gf = g.astype(jnp.float32)
        rows = lax.broadcasted_iota(jnp.int32, (vs, t), 0)
        c0 = (((0,), (0,)), ((), ()))
        c1 = (((1,), (1,)), ((), ()))
        dE = None
        dW = None
        dg = jnp.zeros((d,), jnp.float32)
        us = []
        xs = []
        for k in range(nk):
            oh = (rows == (ids[k] - lo)[None, :]).astype(jnp.bfloat16)
            xp = lax.dot_general(oh, E, c0, preferred_element_type=jnp.float32).astype(jnp.bfloat16)
            x = lax.psum(xp, "tp")
            xf = x.astype(jnp.float32)
            rs = lax.rsqrt(jnp.mean(xf * xf, axis=-1, keepdims=True) + EPS)
            nh = xf * rs
            n = (nh * gf).astype(jnp.bfloat16)
            us.append(jnp.dot(n, W, preferred_element_type=jnp.float32).astype(jnp.bfloat16))
            xs.append(lax.dynamic_slice_in_dim(x, me * ts, ts, 0))
            p = lax.dot_general(du[k], W, c1, preferred_element_type=jnp.float32).astype(jnp.bfloat16)
            got = lax.all_to_all(p.reshape(ntp, ts, d), "tp", 0, 0, tiled=True)
            dn = jnp.sum(got.astype(jnp.float32), axis=0)
            nhl = lax.dynamic_slice_in_dim(nh, me * ts, ts, 0)
            rsl = lax.dynamic_slice_in_dim(rs, me * ts, ts, 0)
            gdn = gf * dn
            dx = dres[k].astype(jnp.float32) + rsl * (gdn - nhl * jnp.mean(nhl * gdn, axis=-1, keepdims=True))
            dg = dg + jnp.sum(dn * nhl, axis=0)
            dxa = lax.all_gather(dx.astype(jnp.bfloat16), "tp", axis=0, tiled=True)
            de = jnp.dot(oh, dxa, preferred_element_type=jnp.float32)
            dE = de if dE is None else dE + de
            dw = lax.dot_general(n, du[k], c0, preferred_element_type=jnp.float32)
            dW = dw if dW is None else dW + dw
        dg = lax.psum(dg, "tp")
        return jnp.stack(us), jnp.stack(xs), dE, dW, dg

    return jax.shard_map(
        body,
        mesh=mesh,
        in_specs=(P("dp", None), P("tp", None), P(None), P(None, "tp"), P("dp", None, "tp"), P("dp", "tp", None)),
        out_specs=(P("dp", None, "tp"), P("dp", "tp", None), P(("dp", "tp"), None), P("dp", "tp"), P("dp")),
        check_vma=False,
    )
```

profile of v0, /device:TPU:0, one launch (start us, length us, event | category | flops | bytes accessed | tf_op | source)
XLA Modules:
  0.0 664.7 jit_solution(6642621581735744870)
XLA Ops:
  17.3 9.4 %convolution_convert_fusion.10 = bf16[256,3072]{1,0:T(8,128)(2,1)} fusion(bf16[2048,3072]{1,0:T(8,128)(2,1)} %param.7, s32[256]{0:T(256)S(1)} %bitcast.168), kind=kOutput, calls=%fused_computation.28 | convolution fusion | flops 3222536192 | bytes 14156800 | tf_op jit(solution)/shard_map/dot_general | solution.py:29
  26.8 9.4 %convolution_convert_fusion.11 = bf16[256,3072]{1,0:T(8,128)(2,1)} fusion(bf16[2048,3072]{1,0:T(8,128)(2,1)} %param.7, s32[256]{0:T(256)S(1)} %bitcast.170), kind=kOutput, calls=%fused_computation.29 | convolution fusion | flops 3222536192 | bytes 14156800 | tf_op jit(solution)/shard_map/dot_general | solution.py:29
  58.2 9.4 %convolution_convert_fusion.15 = bf16[256,3072]{1,0:T(8,128)(2,1)} fusion(bf16[2048,3072]{1,0:T(8,128)(2,1)} %param.7, s32[256]{0:T(256)S(1)} %bitcast.180), kind=kOutput, calls=%fused_computation.33 | convolution fusion | flops 3222536192 | bytes 14156800 | tf_op jit(solution)/shard_map/dot_general | solution.py:29
  71.2 9.3 %convolution_convert_fusion.8 = bf16[256,3072]{1,0:T(8,128)(2,1)} fusion(bf16[2048,3072]{1,0:T(8,128)(2,1)} %param.7, s32[256]{0:T(256)S(1)} %bitcast.182), kind=kOutput, calls=%fused_computation.26 | convolution fusion | flops 3222536192 | bytes 14156800 | tf_op jit(solution)/shard_map/dot_general | solution.py:29
  84.8 9.3 %convolution_convert_fusion.9 = bf16[256,3072]{1,0:T(8,128)(2,1)} fusion(bf16[2048,3072]{1,0:T(8,128)(2,1)} %param.7, s32[256]{0:T(256)S(1)} %bitcast.172), kind=kOutput, calls=%fused_computation.27 | convolution fusion | flops 3222536192 | bytes 14156800 | tf_op jit(solution)/shard_map/dot_general | solution.py:29
  99.0 8.0 %all-to-all-done.4 = bf16[8,32,3072]{2,1,0:T(8,128)(2,1)} async-done(((bf16[8,32,3072]{2,1,0:T(8,128)(2,1)}), bf16[8,32,3072]{2,1,0:T(8,128)(2,1)}, u32[]{:S(2)}, u32[]{:S(2)}) %all-to-all-start.4) | async-done | bytes 1572896 | tf_op jit(solution)/shard_map/all_to_all | solution.py:38
  116.0 33.0 %all-to-all-done.3 = bf16[8,32,3072]{2,1,0:T(8,128)(2,1)} async-done(((bf16[8,32,3072]{2,1,0:T(8,128)(2,1)}), bf16[8,32,3072]{2,1,0:T(8,128)(2,1)}, u32[]{:S(2)}, u32[]{:S(2)}) %all-to-all-start.3) | async-done | bytes 1572896 | tf_op jit(solution)/shard_map/all_to_all | solution.py:38
  158.2 31.6 %all-to-all-done.2 = bf16[8,32,3072]{2,1,0:T(8,128)(2,1)} async-done(((bf16[8,32,3072]{2,1,0:T(8,128)(2,1)}), bf16[8,32,3072]{2,1,0:T(8,128)(2,1)}, u32[]{:S(2)}, u32[]{:S(2)}) %all-to-all-start.2) | async-done | bytes 1572896 | tf_op jit(solution)/shard_map/all_to_all | solution.py:38
  198.9 32.1 %all-to-all-done.1 = bf16[8,32,3072]{2,1,0:T(8,128)(2,1)} async-done(((bf16[8,32,3072]{2,1,0:T(8,128)(2,1)}), bf16[8,32,3072]{2,1,0:T(8,128)(2,1)}, u32[]{:S(2)}, u32[]{:S(2)}) %all-to-all-start.1) | async-done | bytes 1572896 | tf_op jit(solution)/shard_map/all_to_all | solution.py:38
  246.6 23.0 %all-to-all-done = bf16[8,32,3072]{2,1,0:T(8,128)(2,1)} async-done(((bf16[8,32,3072]{2,1,0:T(8,128)(2,1)}), bf16[8,32,3072]{2,1,0:T(8,128)(2,1)}, u32[]{:S(2)}, u32[]{:S(2)}) %all-to-all-start) | async-done | bytes 1572896 | tf_op jit(solution)/shard_map/all_to_all | solution.py:38
  272.0 60.6 %all-reduce.3.cloned.1.call-done = (bf16[256,3072]{1,0:T(8,128)(2,1)}, bf16[256,3072]{1,0:T(8,128)(2,1)}, bf16[256,3072]{1,0:T(8,128)(2,1)}, bf16[256,3072]{1,0:...) async-done(((bf16[256,3072]{1,0:T(8,128)(2,1)}, bf16[256,3072]{1,0:T(8,128)(2,1)}, ...) | async-done | bytes 12582928 | tf_op jit(solution)/shard_map/psum | solution.py:30
  353.8 29.7 %all_to_all.40 = bf16[8,32,3072]{2,1,0:T(8,128)(2,1)S(1)} all-to-all(bf16[8,32,3072]{2,1,0:T(8,128)(2,1)S(1)} %bitcast.167), channel_id=1, replica_groups=mesh['dp'=4,'tp'=8] {'tp'}, dimensions={0} | all-to-all | bytes 3145728 | tf_op jit(solution)/shard_map/all_to_all | solution.py:38
  436.2 5.9 fusion.53
  442.2 22.9 %psum.71 = f32[3072]{0:T(1024)} all-reduce(f32[3072]{0:T(1024)S(1)} %add_add_fusion.2), channel_id=1, replica_groups=mesh['dp'=4,'tp'=8] {'tp'}, use_global_device_ids=true, to_apply=%region_40.0 | all-reduce | flops 3072 | bytes 24576 | tf_op jit(solution)/shard_map/psum | solution.py:50
  466.7 6.3 fusion.47
  492.1 21.5 %add_add_fusion.1 = f32[3072,640]{1,0:T(8,128)} fusion(f32[3072,640]{1,0:T(8,128)} %fusion.53, f32[3072,640]{1,0:T(8,128)} %fusion.52, f32[3072,640]{1,0:T(8,128)} %fusion.51, f32[3072,640]{1,0:T(8,128)} %fusion.50, f32[3072,640]{1,0:T(8,128)} %fusion.49, f32[3072,640]{1,0:T(8,128)} %fusion.47, f32[3072,640]{1,0:T(8,128)} %fusion.48, ...), kind=kOutput, calls=%fused_computation.1 | convolution fusion | flops 1023541248 | bytes 64828416 | tf_op jit(solution)/shard_map/dot_general | solution.py:48
  513.7 11.5 %fusion.14 = f32[2048,3072]{1,0:T(8,128)} fusion(bf16[256,3072]{1,0:T(8,128)(2,1)} %all-gather.9.cloned.1.call-done, s32[256]{0:T(256)S(1)} %bitcast.181), kind=kOutput, calls=%fused_computation.72 | convolution fusion | flops 3221749760 | bytes 26739712 | tf_op jit(solution)/shard_map/dot_general | solution.py:46
  525.2 11.6 %fusion.12 = f32[2048,3072]{1,0:T(8,128)} fusion(bf16[256,3072]{1,0:T(8,128)(2,1)} %all-gather.13.cloned.1.call-done, s32[256]{0:T(256)S(1)} %bitcast.179), kind=kOutput, calls=%fused_computation.68 | convolution fusion | flops 3221749760 | bytes 26739712 | tf_op jit(solution)/shard_map/dot_general | solution.py:46
  536.9 11.5 %fusion.11 = f32[2048,3072]{1,0:T(8,128)} fusion(bf16[256,3072]{1,0:T(8,128)(2,1)} %all-gather.15.cloned.1.call-done, s32[256]{0:T(256)S(1)} %bitcast.177), kind=kOutput, calls=%fused_computation.66 | convolution fusion | flops 3221749760 | bytes 26739712 | tf_op jit(solution)/shard_map/dot_general | solution.py:46
  548.4 11.5 %fusion.13 = f32[2048,3072]{1,0:T(8,128)} fusion(bf16[256,3072]{1,0:T(8,128)(2,1)} %all-gather.11.cloned.1.call-done, s32[256]{0:T(256)S(1)} %bitcast.175), kind=kOutput, calls=%fused_computation.70 | convolution fusion | flops 3221749760 | bytes 26739712 | tf_op jit(solution)/shard_map/dot_general | solution.py:46
  559.9 12.1 %fusion.8 = f32[2048,3072]{1,0:T(8,128)} fusion(bf16[256,3072]{1,0:T(8,128)(2,1)} %all-gather.21.cloned.1.call-done, s32[256]{0:T(256)S(1)} %bitcast.173), kind=kOutput, calls=%fused_computation.60 | convolution fusion | flops 3221749760 | bytes 26739712 | tf_op jit(solution)/shard_map/dot_general | solution.py:46
  572.0 11.5 %fusion.10 = f32[2048,3072]{1,0:T(8,128)} fusion(bf16[256,3072]{1,0:T(8,128)(2,1)} %all-gather.17.cloned.1.call-done, s32[256]{0:T(256)S(1)} %bitcast.171), kind=kOutput, calls=%fused_computation.64 | convolution fusion | flops 3221749760 | bytes 26739712 | tf_op jit(solution)/shard_map/dot_general | solution.py:46
  583.6 11.5 %fusion.9 = f32[2048,3072]{1,0:T(8,128)} fusion(bf16[256,3072]{1,0:T(8,128)(2,1)} %all-gather.19.cloned.1.call-done, s32[256]{0:T(256)S(1)} %bitcast.169), kind=kOutput, calls=%fused_computation.62 | convolution fusion | flops 3221749760 | bytes 26739712 | tf_op jit(solution)/shard_map/dot_general | solution.py:46
  595.1 62.9 %add_add_fusion = f32[2048,3072]{1,0:T(8,128)} fusion(f32[2048,3072]{1,0:T(8,128)} %fusion.8, f32[2048,3072]{1,0:T(8,128)} %fusion.9, f32[2048,3072]{1,0:T(8,128)} %fusion.10, f32[2048,3072]{1,0:T(8,128)} %fusion.11, f32[2048,3072]{1,0:T(8,128)} %fusion.12, f32[2048,3072]{1,0:T(8,128)} %fusion.14, f32[2048,3072]{1,0:T(8,128)} %fusion.13, ...), kind=kOutput, calls=%fused_computation | convolution fusion | flops 3265789952 | bytes 202900480 | tf_op jit(solution)/shard_map/dot_general | solution.py:46
  (293 shorter events, 184.0 us)
Async XLA Ops:
  12.0 41.8 %all-to-all-start.7 = ((bf16[8,32,3072]{2,1,0:T(8,128)(2,1)}), bf16[8,32,3072]{2,1,0:T(8,128)(2,1)S(1)}, u32[]{:S(2)}, u32[]{:S(2)}) async-start(bf16[8,32,3072]{2,1,0:T(8,128)(2,1)} %bitcast.47), calls=%async_computation.7 | async-start | bytes 3145728 | tf_op jit(solution)/shard_map/all_to_all | solution.py:38
  17.3 23.6 %copy-start.51 = (s32[1,256]{1,0:T(1,128)}, s32[1,256]{1,0:T(1,128)S(1)}, u32[]{:S(2)}) copy-start(s32[1,256]{1,0:T(1,128)S(1)} %get-tuple-element.55) | copy-start | bytes 3076
  17.3 31.9 %copy-start.47 = (s32[1,256]{1,0:T(1,128)}, s32[1,256]{1,0:T(1,128)S(1)}, u32[]{:S(2)}) copy-start(s32[1,256]{1,0:T(1,128)S(1)} %get-tuple-element.56) | copy-start | bytes 3076
  17.3 40.9 %copy-start.53 = (s32[1,256]{1,0:T(1,128)}, s32[1,256]{1,0:T(1,128)S(1)}, u32[]{:S(2)}) copy-start(s32[1,256]{1,0:T(1,128)S(1)} %get-tuple-element.57) | copy-start | bytes 3076
  17.3 53.9 %copy-start.70 = (s32[1,256]{1,0:T(1,128)}, s32[1,256]{1,0:T(1,128)S(1)}, u32[]{:S(2)}) copy-start(s32[1,256]{1,0:T(1,128)S(1)} %get-tuple-element.51) | copy-start | bytes 3076
  53.7 26.7 %all-to-all-start.5 = ((bf16[8,32,3072]{2,1,0:T(8,128)(2,1)}), bf16[8,32,3072]{2,1,0:T(8,128)(2,1)S(1)}, u32[]{:S(2)}, u32[]{:S(2)}) async-start(bf16[8,32,3072]{2,1,0:T(8,128)(2,1)} %bitcast.163), calls=%async_computation.5 | async-start | bytes 3145728 | tf_op jit(solution)/shard_map/all_to_all | solution.py:38
  80.4 26.5 %all-to-all-start.4 = ((bf16[8,32,3072]{2,1,0:T(8,128)(2,1)}), bf16[8,32,3072]{2,1,0:T(8,128)(2,1)}, u32[]{:S(2)}, u32[]{:S(2)}) async-start(bf16[8,32,3072]{2,1,0:T(8,128)(2,1)} %bitcast.162), calls=%async_computation.4 | async-start | bytes 3145728 | tf_op jit(solution)/shard_map/all_to_all | solution.py:38
  84.7 247.8 %all-reduce.3.cloned.1.call-start = ((), (), s32[]{:S(2)}) async-start(), calls=%async_computation.16 | async-start | bytes 25165824 | tf_op jit(solution)/shard_map/psum | solution.py:30
  106.9 42.2 %all-to-all-start.3 = ((bf16[8,32,3072]{2,1,0:T(8,128)(2,1)}), bf16[8,32,3072]{2,1,0:T(8,128)(2,1)}, u32[]{:S(2)}, u32[]{:S(2)}) async-start(bf16[8,32,3072]{2,1,0:T(8,128)(2,1)} %bitcast.164), calls=%async_computation.3 | async-start | bytes 3145728 | tf_op jit(solution)/shard_map/all_to_all | solution.py:38
  149.1 40.7 %all-to-all-start.2 = ((bf16[8,32,3072]{2,1,0:T(8,128)(2,1)}), bf16[8,32,3072]{2,1,0:T(8,128)(2,1)}, u32[]{:S(2)}, u32[]{:S(2)}) async-start(bf16[8,32,3072]{2,1,0:T(8,128)(2,1)} %bitcast.165), calls=%async_computation.2 | async-start | bytes 3145728 | tf_op jit(solution)/shard_map/all_to_all | solution.py:38
  189.8 41.2 %all-to-all-start.1 = ((bf16[8,32,3072]{2,1,0:T(8,128)(2,1)}), bf16[8,32,3072]{2,1,0:T(8,128)(2,1)}, u32[]{:S(2)}, u32[]{:S(2)}) async-start(bf16[8,32,3072]{2,1,0:T(8,128)(2,1)} %bitcast.166), calls=%async_computation.1 | async-start | bytes 3145728 | tf_op jit(solution)/shard_map/all_to_all | solution.py:38
  194.1 41.6 %copy-start.73 = (bf16[3072]{0:T(1024)(128)(2,1)S(1)}, bf16[3072]{0:T(1024)(128)(2,1)}, u32[]{:S(2)}) copy-start(bf16[3072]{0:T(1024)(128)(2,1)} %param.8) | copy-start | bytes 18436
  230.9 38.7 %all-to-all-start = ((bf16[8,32,3072]{2,1,0:T(8,128)(2,1)}), bf16[8,32,3072]{2,1,0:T(8,128)(2,1)}, u32[]{:S(2)}, u32[]{:S(2)}) async-start(bf16[8,32,3072]{2,1,0:T(8,128)(2,1)} %bitcast.161), calls=%async_computation | async-start | bytes 3145728 | tf_op jit(solution)/shard_map/all_to_all | solution.py:38
  235.2 278.4 %all-gather.9.cloned.1.call-start = ((), (), s32[]{:S(2)}) async-start(), calls=%async_computation.8 | async-start | bytes 1769472 | tf_op jit(solution)/shard_map/all_gather | solution.py:45
  350.0 175.2 %all-gather.13.cloned.1.call-start = ((), (), s32[]{:S(2)}) async-start(), calls=%async_computation.10 | async-start | bytes 1769472 | tf_op jit(solution)/shard_map/all_gather | solution.py:45
  353.7 30.7 %copy-start.77 = (f32[32]{0:T(128)S(1)}, f32[32]{0:T(128)}, u32[]{:S(2)}) copy-start(f32[32]{0:T(128)} %get-tuple-element.20) | copy-start | bytes 388
  353.7 31.2 %copy-start.74 = (f32[256]{0:T(256)S(1)}, f32[256]{0:T(256)}, u32[]{:S(2)}) copy-start(f32[256]{0:T(256)} %get-tuple-element.66) | copy-start | bytes 3076
  385.6 151.3 %all-gather.15.cloned.1.call-start = ((), (), s32[]{:S(2)}) async-start(), calls=%async_computation.11 | async-start | bytes 1769472 | tf_op jit(solution)/shard_map/all_gather | solution.py:45
  398.6 149.7 %all-gather.11.cloned.1.call-start = ((), (), s32[]{:S(2)}) async-start(), calls=%async_computation.9 | async-start | bytes 1769472 | tf_op jit(solution)/shard_map/all_gather | solution.py:45
  399.2 160.7 %all-gather.21.cloned.1.call-start = ((), (), s32[]{:S(2)}) async-start(), calls=%async_computation.14 | async-start | bytes 1769472 | tf_op jit(solution)/shard_map/all_gather | solution.py:45
  405.8 166.3 %all-gather.17.cloned.1.call-start = ((), (), s32[]{:S(2)}) async-start(), calls=%async_computation.12 | async-start | bytes 1769472 | tf_op jit(solution)/shard_map/all_gather | solution.py:45
  419.3 164.3 %all-gather.19.cloned.1.call-start = ((), (), s32[]{:S(2)}) async-start(), calls=%async_computation.13 | async-start | bytes 1769472 | tf_op jit(solution)/shard_map/all_gather | solution.py:45
  442.1 153.0 %all-gather.23.cloned.1.call-start = ((), (), s32[]{:S(2)}) async-start(), calls=%async_computation.15 | async-start | bytes 1769472 | tf_op jit(solution)/shard_map/all_gather | solution.py:45
  492.1 21.6 %copy-start.54 = (s32[1,256]{1,0:T(1,128)S(1)}, s32[1,256]{1,0:T(1,128)}, u32[]{:S(2)}) copy-start(s32[1,256]{1,0:T(1,128)} %copy-done.53) | copy-start | bytes 3076
  (79 other events, 432.8 us)
Sparse Core Ops, SparseCore 0:
  94.2 238.3 all-reduce.2
  350.1 33.9 all-gather.8
  386.0 25.3 all-gather.12
  413.2 25.3 all-gather.14
  440.3 25.4 all-gather.10
  467.6 25.3 all-gather.20
  494.8 25.2 all-gather.16
  522.0 25.2 all-gather.18
  549.3 25.2 all-gather.22
where the time goes:
time: 675 us; the launch traced here: 665 us
  matrix products  318 us (47%)
  waiting for transfers between devices  189 us (28%)
  blocking collectives  52.6 us (8%)
  other arithmetic  37 us (5%)
  starting transfers between devices  32 us (5%)
  local copies, waits for them, and re-layouts  21.2 us (3%)
  between operations  15 us (2%)
    dot_general x8, matrix products, body(): de = jnp.dot(oh, dxa, preferred_element_type=jnp.float32)  144 us
    all_to_all x7, waiting for transfers between devices, body(): got = lax.all_to_all(p.reshape(ntp, ts, d), 'tp', 0, 0, tiled=True)  128 us
    dot_general x8, matrix products, body(): lax.dot_general(oh, E, c0, preferred_element_type=jnp.float32)  60.7 us
    psum x1, waiting for transfers between devices, body(): x = lax.psum(xp, 'tp')  60.6 us
    dot_general x8, matrix products, body(): dw = lax.dot_general(n, du[k], c0, preferred_element_type=jnp.float32)  58.4 us
    dot_general x8, matrix products, body(): lax.dot_general(du[k], W, c1, preferred_element_type=jnp.float32)  34.9 us
    all_to_all x7, starting transfers between devices, body(): got = lax.all_to_all(p.reshape(ntp, ts, d), 'tp', 0, 0, tiled=True)  31.1 us
    all_to_all x1, blocking collectives, body(): got = lax.all_to_all(p.reshape(ntp, ts, d), 'tp', 0, 0, tiled=True)  29.7 us
  transfers between devices with their start and end apart: 16, of which 6 were waited for; matrix products, arithmetic and copies ran while one was open for 44% of the time, Pallas kernels for 0%

commit v1 on v0

v1 whole, which is shorter than its diff:
```python
import jax
import jax.numpy as jnp
from jax import lax
from jax.sharding import PartitionSpec as P

EPS = 1e-6
CX = 96
CD = 24

C0 = (((0,), (0,)), ((), ()))
C1 = (((1,), (1,)), ((), ()))
F32 = jnp.float32
BF16 = jnp.bfloat16


def rnd(v):
    return lax.reduce_precision(v, 8, 7)


def solution(mesh):
    ntp = mesh.shape["tp"]

    def pp(v, j):
        return lax.ppermute(v, "tp", [(i, i ^ j) for i in range(ntp)])

    def grad_dx(dn, xl, gf, dresl):
        xf = xl.astype(F32)
        rs = lax.rsqrt(jnp.mean(xf * xf, axis=-1, keepdims=True) + EPS)
        nh = xf * rs
        gdn = gf * dn
        dx = dresl.astype(F32) + rs * (gdn - nh * jnp.mean(nh * gdn, axis=-1, keepdims=True))
        dg = jnp.sum(dn * nh, axis=0)
        return dx.astype(BF16), dg

    def body(ids, E, g, W, du, dres):
        vs, d = E.shape
        nk, t = ids.shape
        ts = t // ntp
        nt = nk * t
        fs = W.shape[1]
        h = d // 2
        me = lax.axis_index("tp")
        core = me & 1
        chip = me >> 1
        lo = me * vs
        gf = g.astype(F32)

        idf = ids.reshape(nt)
        own = idf // vs
        tok = jnp.arange(nt, dtype=jnp.int32)
        big = jnp.int32(1 << 20)
        eq = idf[:, None] == idf[None, :]
        first = jnp.min(jnp.where(eq, tok[:, None], big), axis=0)
        isf = first == tok
        slot = jnp.sum(
            (isf[:, None] & (own[:, None] == own[None, :]) & (tok[:, None] < first[None, :])).astype(jnp.int32), axis=0
        )
        idl = ids.reshape(nk, ntp, ts).transpose(1, 0, 2).reshape(ntp, nk * ts)
        ownl = idl // vs
        tl = jnp.arange(nk * ts, dtype=jnp.int32)
        eql = idl[:, :, None] == idl[:, None, :]
        firstl = jnp.min(jnp.where(eql, tl[None, :, None], big), axis=1)
        isfl = firstl == tl[None, :]
        slotl = jnp.sum(
            (
                isfl[:, :, None] & (ownl[:, :, None] == ownl[:, None, :]) & (tl[None, :, None] < firstl[:, None, :])
            ).astype(jnp.int32),
            axis=1,
        )
        over = (jnp.max(slot) >= CX) | (jnp.max(slotl) >= CD)

        def rel(o):
            return ((o ^ me) & 1) * (ntp // 2) + ((o ^ me) >> 1)

        duv = du.reshape(nk, ntp // 2, 2, ts, fs)
        dum = lax.dynamic_index_in_dim(duv, core, 2, keepdims=False)
        dut = lax.dynamic_index_in_dim(duv, 1 - core, 2, keepdims=False)
        dus = pp(dut, 1)
        ws = pp(W, 1)

        def fast(ids, E, g, W, du, dres, ws, dus, dum):
            row_of = jnp.max(
                jnp.where(
                    (own == me)[:, None] & (slot[:, None] == jnp.arange(CX, dtype=jnp.int32)[None, :]),
                    (idf - lo)[:, None],
                    -1,
                ),
                axis=0,
            )
            ohe = (row_of[:, None] == lax.broadcasted_iota(jnp.int32, (CX, vs), 1)).astype(BF16)
            xc = jnp.dot(ohe, E, preferred_element_type=F32).astype(BF16)
            hc = CX // 2
            px = pp(xc, 2)
            py = pp(xc, 4)
            dlo = pp(px[:hc], 4)
            dhi = pp(py[hc:], 2)
            xh = jnp.concatenate([xc, px, py, dlo, dhi], axis=0)
            xall = jnp.concatenate([xh, pp(xh, 1)], axis=0)
            xf = xall.astype(F32)
            rs = lax.rsqrt(jnp.mean(xf * xf, axis=-1, keepdims=True) + EPS)
            nc = (xf * rs * gf).astype(BF16)
            gpos = rel(own) * CX + slot
            oh = (gpos[:, None] == lax.broadcasted_iota(jnp.int32, (nt, ntp * CX), 1)).astype(BF16)
            n = jnp.dot(oh, nc, preferred_element_type=F32).astype(BF16)
            u = jnp.dot(n, W, preferred_element_type=F32).astype(BF16).reshape(nk, t, fs)
            dW = lax.dot_general(n, du.reshape(nt, fs), C0, preferred_element_type=F32)
            ohl = lax.dynamic_slice_in_dim(oh.reshape(nk, t, ntp * CX), me * ts, ts, 1).reshape(nk * ts, ntp * CX)
            xl = jnp.dot(ohl, xall, preferred_element_type=F32).astype(BF16)

            def p2(k):
                q = chip ^ k
                a = lax.dynamic_index_in_dim(dum, q, 1, keepdims=False).reshape(nk * ts, fs)
                b = lax.dynamic_index_in_dim(dus, q, 1, keepdims=False).reshape(nk * ts, fs)
                pa = rnd(lax.dot_general(a, W, C1, preferred_element_type=F32))
                pb = rnd(lax.dot_general(b, ws, C1, preferred_element_type=F32))
                return pa + pb

            p3 = p2(3)
            r2 = pp(p3[:, :h], 2)
            r1 = pp(p3[:, h:], 4)
            p1 = p2(1)
            p2_ = p2(2)
            ax = pp(p1[:, :h], 2)
            ay = pp(p2_[:, h:], 4)
            p0 = p2(0)
            by = pp(p2_[:, :h] + r2, 4)
            bx = pp(p1[:, h:] + r1, 2)
            dn = jnp.concatenate([p0[:, :h] + ax + by, p0[:, h:] + ay + bx], axis=1)

            dxb, dg = grad_dx(dn, xl, gf, dres.reshape(nk * ts, d))
            for j in (1, 2, 4):
                dg = dg + pp(dg, j)

            idm = lax.dynamic_index_in_dim(idl, me, 0, keepdims=False)
            om = idm // vs
            sm = lax.dynamic_index_in_dim(slotl, me, 0, keepdims=False)
            pm = (om ^ me) * CD + sm
            ohm = (lax.broadcasted_iota(jnp.int32, (ntp * CD, nk * ts), 0) == pm[None, :]).astype(BF16)
            rows = jnp.dot(ohm, dxb, preferred_element_type=F32).reshape(ntp, CD, d)
            got = jnp.concatenate([rows[0]] + [pp(rows[j], j) for j in range(1, ntp)], axis=0)
            vr = jnp.max(
                jnp.where(
                    (ownl == me)[:, :, None] & (slotl[:, :, None] == jnp.arange(CD, dtype=jnp.int32)[None, None, :]),
                    (idl - lo)[:, :, None],
                    -1,
                ),
                axis=1,
            )
            vr = jnp.take(vr, jnp.arange(ntp, dtype=jnp.int32) ^ me, axis=0).reshape(ntp * CD)
            s1 = rnd(got)
            e1 = got - s1
            s2 = rnd(e1)
            s3 = e1 - s2
            sp = jnp.concatenate([s1.astype(BF16), s2.astype(BF16), s3.astype(BF16)], axis=0)
            vr3 = jnp.concatenate([vr, vr, vr], axis=0)
            ohd = (lax.broadcasted_iota(jnp.int32, (vs, 3 * ntp * CD), 0) == vr3[None, :]).astype(BF16)
            dE = jnp.dot(ohd, sp, preferred_element_type=F32)
            return u, xl.reshape(nk, ts, d), dE, dW, dg

        def slow(ids, E, g, W, du, dres, ws, dus, dum):
            oh = (lax.broadcasted_iota(jnp.int32, (vs, nt), 0) == (idf - lo)[None, :]).astype(BF16)
            x = lax.dot_general(oh, E, C0, preferred_element_type=F32).astype(BF16)
            for j in (1, 2, 4):
                x = x + pp(x, j)
            xf = x.astype(F32)
            rs = lax.rsqrt(jnp.mean(xf * xf, axis=-1, keepdims=True) + EPS)
            n = (xf * rs * gf).astype(BF16)
            u = jnp.dot(n, W, preferred_element_type=F32).astype(BF16).reshape(nk, t, fs)
            dW = lax.dot_general(n, du.reshape(nt, fs), C0, preferred_element_type=F32)
            xl = lax.dynamic_slice_in_dim(x.reshape(nk, t, d), me * ts, ts, 1).reshape(nk * ts, d)
            p = lax.dot_general(du.reshape(nt, fs), W, C1, preferred_element_type=F32).astype(BF16)
            p = p.reshape(nk, ntp, ts, d)
            dn = jnp.zeros((nk * ts, d), F32)
            for j in range(ntp):
                q = lax.dynamic_index_in_dim(p, me ^ j, 1, keepdims=False).reshape(nk * ts, d)
                if j:
                    q = pp(q, j)
                dn = dn + q.astype(F32)
            dxb, dg = grad_dx(dn, xl, gf, dres.reshape(nk * ts, d))
            for j in (1, 2, 4):
                dg = dg + pp(dg, j)
            dE = jnp.zeros((vs, d), F32)
            for j in range(ntp):
                q = pp(dxb, j) if j else dxb
                iq = lax.dynamic_index_in_dim(idl, me ^ j, 0, keepdims=False)
                ohq = (lax.broadcasted_iota(jnp.int32, (vs, nk * ts), 0) == (iq - lo)[None, :]).astype(BF16)
                dE = dE + jnp.dot(ohq, q, preferred_element_type=F32)
            return u, xl.reshape(nk, ts, d), dE, dW, dg

        return lax.cond(over, slow, fast, ids, E, g, W, du, dres, ws, dus, dum)

    return jax.shard_map(
        body,
        mesh=mesh,
        in_specs=(P("dp", None), P("tp", None), P(None), P(None, "tp"), P("dp", None, "tp"), P("dp", "tp", None)),
        out_specs=(P("dp", None, "tp"), P("dp", "tp", None), P(("dp", "tp"), None), P("dp", "tp"), P("dp")),
        check_vma=False,
    )
```

time: 675 us -> 267 us (0.40)
  matrix products: 318 us -> 88.9 us
  waiting for transfers between devices: 189 us -> 96.3 us
  blocking collectives: 52.6 us -> 0 us
  between operations: 15 us -> 3.16 us
  other arithmetic: 37 us -> 25.6 us
  starting transfers between devices: 32 us -> 21.2 us
  loops' own time: 0 us -> 7.92 us
    dot_general x40 -> x15, matrix products: 318 us -> 88.9 us  [the longest x4 15.9 us: p2(): pb = rnd(lax.dot_general(b, ws, C1, preferred_element_type=F32))]
    all_to_all x7 -> x0, waiting for transfers between devices: 128 us -> none  [body(): got = lax.all_to_all(p.reshape(ntp, ts, d), 'tp', 0, 0, tiled=True)]
    ppermute x0 -> x23, waiting for transfers between devices: none -> 96.3 us  [pp(): return lax.ppermute(v, 'tp', [(i, i ^ j) for i in range(ntp)])]
    psum x1 -> x0, waiting for transfers between devices: 60.6 us -> none  [body(): x = lax.psum(xp, 'tp')]
    all_to_all x7 -> x0, starting transfers between devices: 31.1 us -> none  [body(): got = lax.all_to_all(p.reshape(ntp, ts, d), 'tp', 0, 0, tiled=True)]
    all_to_all x1 -> x0, blocking collectives: 29.7 us -> none  [body(): got = lax.all_to_all(p.reshape(ntp, ts, d), 'tp', 0, 0, tiled=True)]
    psum x1 -> x0, blocking collectives: 22.9 us -> none  [body(): dg = lax.psum(dg, 'tp')]
    ppermute x0 -> x23, starting transfers between devices: none -> 21.2 us  [pp(): return lax.ppermute(v, 'tp', [(i, i ^ j) for i in range(ntp)])]
  transfers between devices with their start and end apart: 16 -> 23, of which waited for: 6 -> 7; matrix products, arithmetic and copies ran while one was open for 44% -> 40% of each run, Pallas kernels for 0% -> 0%
where the time goes in v1:
time: 267 us; the launch traced here: 262 us
  waiting for transfers between devices  96.3 us (36%)
  matrix products  88.9 us (33%)
  other arithmetic  25.6 us (10%)
  starting transfers between devices  21.2 us (8%)
  local copies, waits for them, and re-layouts  19.4 us (7%)
  loops' own time  7.92 us (3%)
  between operations  3.16 us (1%)
    ppermute x23, waiting for transfers between devices, pp(): return lax.ppermute(v, 'tp', [(i, i ^ j) for i in range(ntp)])  96.3 us
    ppermute x23, starting transfers between devices, pp(): return lax.ppermute(v, 'tp', [(i, i ^ j) for i in range(ntp)])  21.2 us
    dot_general x4, matrix products, p2(): pb = rnd(lax.dot_general(b, ws, C1, preferred_element_type=F32))  15.9 us
    dot_general x1, matrix products, fast(): jnp.dot(n, W, preferred_element_type=F32).astype(BF16).reshape(nk, t, fs)  15.2 us
    dot_general x1, matrix products, fast(): n = jnp.dot(oh, nc, preferred_element_type=F32).astype(BF16)  13.5 us
    dot_general x1, matrix products, fast(): dE = jnp.dot(ohd, sp, preferred_element_type=F32)  13.3 us
    dot_general x1, matrix products, fast(): dW = lax.dot_general(n, du.reshape(nt, fs), C0, preferred_element_type=F32)  12.9 us
    dot_general x4, matrix products, p2(): pa = rnd(lax.dot_general(a, W, C1, preferred_element_type=F32))  8.11 us
  transfers between devices with their start and end apart: 23, of which 7 were waited for; matrix products, arithmetic and copies ran while one was open for 40% of the time, Pallas kernels for 0%

profile of v1, /device:TPU:0, one launch (start us, length us, event | category | flops | bytes accessed | tf_op | source)
XLA Modules:
  0.0 262.5 jit_solution(5522110708786568919)
XLA Ops:
  3.5 2.3 select_reduce_fusion.2
  5.8 4.6 %convert_reduce_fusion = s32[2048]{0:T(1024)S(1)} fusion(s32[2048]{0:T(1024)S(1)} %select_reduce_fusion.2, s32[2048]{0:T(1024)S(1)} %get-tuple-element.222, pred[2048]{0:T(1024)(128)(4,1)S(1)} %iota_compare_fusion.34), kind=kLoop, calls=%fused_computation.211 | loop fusion | flops 25163776 | bytes 26624 | tf_op jit(solution)/shard_map/reduce_sum | solution.py:55
  15.9 245.5 %conditional.1 = (bf16[8,256,640]{2,1,0:T(8,128)(2,1)}, bf16[8,32,3072]{2,1,0:T(8,128)(2,1)}, f32[2048,3072]{1,0:T(8,128)}, f32[3072,640]{1,0:T(8,128)}, f32[3072]{0:T(1024)}) conditional(s32[]{:T(128)} %convert_element_type.126, (s32[2048]{0:T(1024)S(1)}, s32[2048]{0:T(1024)S(1)}, pred[2048]{0:T(1024)(128)(4,1)S(1)}, s32[2048]{0:T(1024)S(1)}, ...), branch_computations={%region_6.13_spmd, %region_13.18_spmd} | conditional | flops 75879940096 | bytes 1039036224 | solution.py:190
  16.4 8.0 %constant_dynamic-update-slice_fusion.4 = (bf16[384,3072]{1,0:T(8,128)(2,1)}, bf16[768,3072]{1,0:T(8,128)(2,1)}, bf16[96,3072]{1,0:T(8,128)(2,1)}) fusion(bf16[2048,3072]{1,0:T(8,128)(2,1)} %get-tuple-element.115, s32[96]{0:T(128)S(1)} %select_reduce_fusion), kind=kOutput, calls=%fused_computation.155 | convolution fusion | flops 1208451072 | bytes 14352768 | tf_op jit(solution)/shard_map/cond/branch_0_fun/dot_general | solution.py:91
  24.4 3.0 %collective-permute-start.1 = (bf16[96,3072]{1,0:T(8,128)(2,1)}, bf16[96,3072]{1,0:T(8,128)(2,1)}, u32[]{:S(2)}, u32[]{:S(2)}) collective-permute-start(bf16[96,3072]{1,0:T(8,128)(2,1)} %get-tuple-element.214), channel_id=1, source_target_pairs={{0,4},{1,5},{2,6},{3,7},{4,0},{5,1},{6,2},{7,3},{8,12},{9,13},{10,... | collective-permute-start | bytes 1769480 | tf_op jit(solution)/shard_map/cond/branch_0_fun/ppermute | solution.py:24
  29.0 2.3 constant_dynamic-slice_fusion.24
  32.8 3.5 %fusion.51 = f32[256,3072]{1,0:T(8,128)S(1)} fusion(f32[256,3072]{1,0:T(8,128)S(1)} %convolution_reduce-precision_fusion.1, bf16[256,640]{1,0:T(8,128)(2,1)S(1)} %bitcast.118, bf16[3072,640]{1,0:T(8,128)(2,1)} %get-tuple-element.128), kind=kOutput, calls=%fused_computation.93 | convolution fusion | flops 1008205824 | bytes 10551296 | tf_op jit(solution)/shard_map/cond/branch_0_fun/dot_general | solution.py:115
  41.7 5.2 %fusion.52 = f32[256,3072]{1,0:T(8,128)} fusion(f32[256,3072]{1,0:T(8,128)S(1)} %convolution_reduce-precision_fusion.3, bf16[256,640]{1,0:T(8,128)(2,1)S(1)} %bitcast.115, bf16[3072,640]{1,0:T(8,128)(2,1)} %get-tuple-element.128), kind=kOutput, calls=%fused_computation.96 | convolution fusion | flops 1008205824 | bytes 10551296 | tf_op jit(solution)/shard_map/cond/branch_0_fun/dot_general | solution.py:115
  47.1 3.5 %fusion.53 = f32[256,3072]{1,0:T(8,128)S(1)} fusion(f32[256,3072]{1,0:T(8,128)S(1)} %convolution_reduce-precision_fusion.5, bf16[256,640]{1,0:T(8,128)(2,1)S(1)} %bitcast.114, bf16[3072,640]{1,0:T(8,128)(2,1)} %get-tuple-element.128), kind=kOutput, calls=%fused_computation.99 | convolution fusion | flops 1008205824 | bytes 10551296 | tf_op jit(solution)/shard_map/cond/branch_0_fun/dot_general | solution.py:115
  61.5 19.5 %collective-permute-done.2 = bf16[48,3072]{1,0:T(8,128)(2,1)S(1)} collective-permute-done((bf16[48,3072]{1,0:T(8,128)(2,1)S(1)}, bf16[48,3072]{1,0:T(8,128)(2,1)S(1)}, u32[]{:S(2)}, u32[]{:S(2)}) %collective-permute-start.2) | collective-permute-done | bytes 294944 | tf_op jit(solution)/shard_map/cond/branch_0_fun/ppermute | solution.py:24
  83.3 3.5 %slice_add_fusion.2 = (f32[256,1536]{1,0:T(8,128)}, f32[256,1536]{1,0:T(8,128)}) fusion(f32[256,1536]{1,0:T(8,128)} %collective-permute-done.6, f32[256,3072]{1,0:T(8,128)S(1)} %copy-done.7), kind=kLoop, calls=%fused_computation.135 | loop fusion | flops 393216 | bytes 7864320 | tf_op jit(solution)/shard_map/cond/branch_0_fun/add | solution.py:126
  88.8 3.5 %fusion.97 = (f32[256,1536]{1,0:T(8,128)}, f32[256,1536]{1,0:T(8,128)}) fusion(f32[256,3072]{1,0:T(8,128)S(1)} %fusion.53, f32[256,1536]{1,0:T(8,128)} %collective-permute-done.9), kind=kLoop, calls=%fused_computation.241 | loop fusion | flops 393216 | bytes 7864320 | tf_op jit(solution)/shard_map/cond/branch_0_fun/slice | solution.py:123
  94.8 3.9 %convolution_reduce-precision_fusion.7 = f32[256,3072]{1,0:T(8,128)S(1)} fusion(bf16[256,640]{1,0:T(8,128)(2,1)} %bitcast.113, bf16[3072,640]{1,0:T(8,128)(2,1)} %get-tuple-element.117), kind=kOutput, calls=%fused_computation.103 | convolution fusion | flops 1007419392 | bytes 7405568 | tf_op jit(solution)/shard_map/cond/branch_0_fun/dot_general | solution.py:114
  98.7 3.7 %fusion.54 = f32[256,3072]{1,0:T(8,128)S(1)} fusion(f32[256,3072]{1,0:T(8,128)S(1)} %convolution_reduce-precision_fusion.7, bf16[256,640]{1,0:T(8,128)(2,1)S(1)} %bitcast.112, bf16[3072,640]{1,0:T(8,128)(2,1)} %get-tuple-element.128), kind=kOutput, calls=%fused_computation.102 | convolution fusion | flops 1008205824 | bytes 10551296 | tf_op jit(solution)/shard_map/cond/branch_0_fun/dot_general | solution.py:115
  102.4 21.6 %collective-permute-done.7 = f32[256,1536]{1,0:T(8,128)} collective-permute-done((f32[256,1536]{1,0:T(8,128)}, f32[256,1536]{1,0:T(8,128)}, u32[]{:S(2)}, u32[]{:S(2)}) %collective-permute-start.7) | collective-permute-done | bytes 1572896 | tf_op jit(solution)/shard_map/cond/branch_0_fun/ppermute | solution.py:24
  124.1 33.2 %collective-permute-done.8 = f32[256,1536]{1,0:T(8,128)} collective-permute-done((f32[256,1536]{1,0:T(8,128)}, f32[256,1536]{1,0:T(8,128)}, u32[]{:S(2)}, u32[]{:S(2)}) %collective-permute-start.8) | collective-permute-done | bytes 1572896 | tf_op jit(solution)/shard_map/cond/branch_0_fun/ppermute | solution.py:24
  157.3 4.9 %collective-permute-done.10 = f32[256,1536]{1,0:T(8,128)S(1)} collective-permute-done((f32[256,1536]{1,0:T(8,128)}, f32[256,1536]{1,0:T(8,128)S(1)}, u32[]{:S(2)}, u32[]{:S(2)}) %collective-permute-start.10) | collective-permute-done | bytes 1572896 | tf_op jit(solution)/shard_map/cond/branch_0_fun/ppermute | solution.py:24
  162.2 2.9 %fusion.74 = (f32[256,1536]{1,0:T(8,128)S(1)}, f32[256,1536]{1,0:T(8,128)S(1)}) fusion(f32[256,1536]{1,0:T(8,128)} %collective-permute-done.7, f32[256,1536]{1,0:T(8,128)S(1)} %collective-permute-done.5, f32[256,3072]{1,0:T(8,128)S(1)} %fusion.54, f32[256,1536]{1,0:T(8,128)S(1)} %collective-permute-done.10, f32[256,1536]{1,0:T(8,128)} %collective-permute-done.8), kind=kLoop, calls=%fused_computation.137 | loop fusion | flops 1572864 | bytes 12582912 | tf_op jit(solution)/shard_map/cond/branch_0_fun/add | solution.py:128
  177.0 13.5 %convolution_convert_fusion.1 = bf16[2048,3072]{1,0:T(8,128)(2,1)} fusion(bf16[768,3072]{1,0:T(8,128)(2,1)S(1)} %constant_dynamic-update-slice_fusion.5, f32[3072]{0:T(1024)S(1)} %get-tuple-element.116, f32[768]{0:T(1024)S(1)} %add_rsqrt_fusion.2, s32[2048]{0:T(1024)S(1)} %get-tuple-element.158), kind=kOutput, calls=%fused_computation.83 | convolution fusion | flops 9680977920 | bytes 17325056 | tf_op jit(solution)/shard_map/cond/branch_0_fun/dot_general | solution.py:104
  192.2 15.2 %convolution_convert_fusion.4 = bf16[2048,640]{1,0:T(8,128)(2,1)} fusion(bf16[2048,3072]{1,0:T(8,128)(2,1)} %convolution_convert_fusion.1, bf16[3072,640]{1,0:T(8,128)(2,1)S(1)} %copy-done.1), kind=kOutput, calls=%fused_computation.120 | convolution fusion | flops 8054374400 | bytes 19136512 | tf_op jit(solution)/shard_map/cond/branch_0_fun/dot_general | solution.py:105
  208.3 12.9 %fusion.100 = f32[3072,640]{1,0:T(8,128)} fusion(bf16[2048,3072]{1,0:T(8,128)(2,1)S(1)} %bitcast.140, bf16[2048,640]{1,0:T(8,128)(2,1)S(1)} %bitcast.106), kind=kOutput, calls=%fused_computation.244 | convolution fusion | flops 8053063680 | bytes 23068672 | tf_op jit(solution)/shard_map/cond/branch_0_fun/dot_general | solution.py:106
  223.5 8.0 %collective-permute-done.12 = f32[24,3072]{1,0:T(8,128)S(1)} collective-permute-done((f32[24,3072]{1,0:T(8,128)S(1)}, f32[24,3072]{1,0:T(8,128)S(1)}, u32[]{:S(2)}, u32[]{:S(2)}) %collective-permute-start.12) | collective-permute-done | bytes 294944 | tf_op jit(solution)/shard_map/cond/branch_0_fun/ppermute | solution.py:24
  231.6 8.4 %collective-permute-done.13 = f32[24,3072]{1,0:T(8,128)S(1)} collective-permute-done((f32[24,3072]{1,0:T(8,128)S(1)}, f32[24,3072]{1,0:T(8,128)S(1)}, u32[]{:S(2)}, u32[]{:S(2)}) %collective-permute-start.13) | collective-permute-done | bytes 294944 | tf_op jit(solution)/shard_map/cond/branch_0_fun/ppermute | solution.py:24
  240.8 13.3 %fusion.47 = f32[2048,3072]{1,0:T(8,128)} fusion(bf16[192,3072]{1,0:T(8,128)(2,1)S(1)} %get-tuple-element.189, bf16[192,3072]{1,0:T(8,128)(2,1)S(1)} %get-tuple-element.190, bf16[192,3072]{1,0:T(8,128)(2,1)S(1)} %get-tuple-element.188, s32[576]{0:T(1024)S(1)} %pad_add_fusion), kind=kOutput, calls=%fused_computation.89 | convolution fusion | flops 7259553792 | bytes 28707072 | tf_op jit(solution)/shard_map/cond/branch_0_fun/dot_general | solution.py:157
  (130 shorter events, 51.0 us)
Async XLA Ops:
  0.6 15.3 %collective-permute-start.42 = (bf16[3072,640]{1,0:T(8,128)(2,1)}, bf16[3072,640]{1,0:T(8,128)(2,1)}, u32[]{:S(2)}, u32[]{:S(2)}) collective-permute-start(bf16[3072,640]{1,0:T(8,128)(2,1)} %param.11), channel_id=1, source_target_pairs={{0,1},{1,0},{2,3},{3,2},{4,5},{5,4},{6,7},{7,6},{8,9},{9,8},{10,11... | collective-permute-start | bytes 11796488 | tf_op jit(solution)/shard_map/ppermute | solution.py:24
  2.7 13.2 %collective-permute-start.41 = (bf16[8,4,32,640]{3,2,1,0:T(8,128)(2,1)S(1)}, bf16[8,4,32,640]{3,2,1,0:T(8,128)(2,1)S(1)}, u32[]{:S(2)}, u32[]{:S(2)}) collective-permute-start(bf16[8,4,32,640]{3,2,1,0:T(8,128)(2,1)S(1)} %dynamic-slice_bitcast_fusion), channel_id=1, source_target_pairs={{0,1},{1,0},{2,3},{3,2},{4,5},{5,4},{6,7},{7,6},{8,9},{9,8},{10,11... | collective-permute-start | bytes 3932168 | tf_op jit(solution)/shard_map/ppermute | solution.py:24
  24.4 26.9 %collective-permute-start.1 = (bf16[96,3072]{1,0:T(8,128)(2,1)}, bf16[96,3072]{1,0:T(8,128)(2,1)}, u32[]{:S(2)}, u32[]{:S(2)}) collective-permute-start(bf16[96,3072]{1,0:T(8,128)(2,1)} %get-tuple-element.214), channel_id=1, source_target_pairs={{0,4},{1,5},{2,6},{3,7},{4,0},{5,1},{6,2},{7,3},{8,12},{9,13},{10,... | collective-permute-start | bytes 1769480 | tf_op jit(solution)/shard_map/cond/branch_0_fun/ppermute | solution.py:24
  27.4 27.1 %collective-permute-start = (bf16[96,3072]{1,0:T(8,128)(2,1)}, bf16[96,3072]{1,0:T(8,128)(2,1)}, u32[]{:S(2)}, u32[]{:S(2)}) collective-permute-start(bf16[96,3072]{1,0:T(8,128)(2,1)} %get-tuple-element.214), channel_id=1, source_target_pairs={{0,2},{1,3},{2,0},{3,1},{4,6},{5,7},{6,4},{7,5},{8,10},{9,11},{10,... | collective-permute-start | bytes 1769480 | tf_op jit(solution)/shard_map/cond/branch_0_fun/ppermute | solution.py:24
  38.3 45.0 %collective-permute-start.6 = (f32[256,1536]{1,0:T(8,128)}, f32[256,1536]{1,0:T(8,128)}, u32[]{:S(2)}, u32[]{:S(2)}) collective-permute-start(f32[256,1536]{1,0:T(8,128)} %get-tuple-element.182), channel_id=1, source_target_pairs={{0,2},{1,3},{2,0},{3,1},{4,6},{5,7},{6,4},{7,5},{8,10},{9,11},{10,... | collective-permute-start | bytes 4718600 | tf_op jit(solution)/shard_map/cond/branch_0_fun/ppermute | solution.py:24
  38.8 50.0 %collective-permute-start.9 = (f32[256,1536]{1,0:T(8,128)}, f32[256,1536]{1,0:T(8,128)}, u32[]{:S(2)}, u32[]{:S(2)}) collective-permute-start(f32[256,1536]{1,0:T(8,128)} %get-tuple-element.183), channel_id=1, source_target_pairs={{0,4},{1,5},{2,6},{3,7},{4,0},{5,1},{6,2},{7,3},{8,12},{9,13},{10,... | collective-permute-start | bytes 4718600 | tf_op jit(solution)/shard_map/cond/branch_0_fun/ppermute | solution.py:24
  52.4 30.0 %collective-permute-start.3 = (bf16[48,3072]{1,0:T(8,128)(2,1)S(1)}, bf16[48,3072]{1,0:T(8,128)(2,1)S(1)}, u32[]{:S(2)}, u32[]{:S(2)}) collective-permute-start(bf16[48,3072]{1,0:T(8,128)(2,1)S(1)} %slice.65), channel_id=1, source_target_pairs={{0,2},{1,3},{2,0},{3,1},{4,6},{5,7},{6,4},{7,5},{8,10},{9,11},{10,... | collective-permute-start | bytes 884744 | tf_op jit(solution)/shard_map/cond/branch_0_fun/ppermute | solution.py:24
  55.5 25.5 %collective-permute-start.2 = (bf16[48,3072]{1,0:T(8,128)(2,1)S(1)}, bf16[48,3072]{1,0:T(8,128)(2,1)S(1)}, u32[]{:S(2)}, u32[]{:S(2)}) collective-permute-start(bf16[48,3072]{1,0:T(8,128)(2,1)S(1)} %slice.64), channel_id=1, source_target_pairs={{0,4},{1,5},{2,6},{3,7},{4,0},{5,1},{6,2},{7,3},{8,12},{9,13},{10,... | collective-permute-start | bytes 884744 | tf_op jit(solution)/shard_map/cond/branch_0_fun/ppermute | solution.py:24
  83.3 81.8 %collective-permute-start.4 = (bf16[384,3072]{1,0:T(8,128)(2,1)}, bf16[384,3072]{1,0:T(8,128)(2,1)}, u32[]{:S(2)}, u32[]{:S(2)}) collective-permute-start(bf16[384,3072]{1,0:T(8,128)(2,1)} %get-tuple-element.209), channel_id=1, source_target_pairs={{0,1},{1,0},{2,3},{3,2},{4,5},{5,4},{6,7},{7,6},{8,9},{9,8},{10,11... | collective-permute-start | bytes 7077896 | tf_op jit(solution)/shard_map/cond/branch_0_fun/ppermute | solution.py:24
  86.8 37.3 %collective-permute-start.7 = (f32[256,1536]{1,0:T(8,128)}, f32[256,1536]{1,0:T(8,128)}, u32[]{:S(2)}, u32[]{:S(2)}) collective-permute-start(f32[256,1536]{1,0:T(8,128)} %get-tuple-element.180), channel_id=1, source_target_pairs={{0,4},{1,5},{2,6},{3,7},{4,0},{5,1},{6,2},{7,3},{8,12},{9,13},{10,... | collective-permute-start | bytes 4718600 | tf_op jit(solution)/shard_map/cond/branch_0_fun/ppermute | solution.py:24
  87.9 69.4 %collective-permute-start.8 = (f32[256,1536]{1,0:T(8,128)}, f32[256,1536]{1,0:T(8,128)}, u32[]{:S(2)}, u32[]{:S(2)}) collective-permute-start(f32[256,1536]{1,0:T(8,128)} %get-tuple-element.181), channel_id=1, source_target_pairs={{0,4},{1,5},{2,6},{3,7},{4,0},{5,1},{6,2},{7,3},{8,12},{9,13},{10,... | collective-permute-start | bytes 4718600 | tf_op jit(solution)/shard_map/cond/branch_0_fun/ppermute | solution.py:24
  92.3 65.0 %collective-permute-start.5 = (f32[256,1536]{1,0:T(8,128)}, f32[256,1536]{1,0:T(8,128)S(1)}, u32[]{:S(2)}, u32[]{:S(2)}) collective-permute-start(f32[256,1536]{1,0:T(8,128)} %get-tuple-element.178), channel_id=1, source_target_pairs={{0,2},{1,3},{2,0},{3,1},{4,6},{5,7},{6,4},{7,5},{8,10},{9,11},{10,... | collective-permute-start | bytes 4718600 | tf_op jit(solution)/shard_map/cond/branch_0_fun/ppermute | solution.py:24
  93.8 68.5 %collective-permute-start.10 = (f32[256,1536]{1,0:T(8,128)}, f32[256,1536]{1,0:T(8,128)S(1)}, u32[]{:S(2)}, u32[]{:S(2)}) collective-permute-start(f32[256,1536]{1,0:T(8,128)} %get-tuple-element.179), channel_id=1, source_target_pairs={{0,2},{1,3},{2,0},{3,1},{4,6},{5,7},{6,4},{7,5},{8,10},{9,11},{10,... | collective-permute-start | bytes 4718600 | tf_op jit(solution)/shard_map/cond/branch_0_fun/ppermute | solution.py:24
  98.7 66.4 %slice-start = ((s8[4718592]{0:T(1024)(128)(4,1)}), s8[4194304]{0:T(1024)(128)(4,1)S(1)}, s32[]{:S(2)}) async-start(s8[4718592]{0:T(1024)(128)(4,1)} %bitcast.101), calls=%async_computation | async-start | bytes 8388608 | tf_op jit(solution)/shard_map/cond
  170.6 19.9 %collective-permute-start.18 = (f32[3072]{0:T(1024)S(1)}, f32[3072]{0:T(1024)S(1)}, u32[]{:S(2)}, u32[]{:S(2)}) collective-permute-start(f32[3072]{0:T(1024)S(1)} %get-tuple-element.151), channel_id=1, source_target_pairs={{0,1},{1,0},{2,3},{3,2},{4,5},{5,4},{6,7},{7,6},{8,9},{9,8},{10,11... | collective-permute-start | bytes 36872 | tf_op jit(solution)/shard_map/cond/branch_0_fun/ppermute | solution.py:24
  173.4 66.7 %collective-permute-start.17 = (f32[24,3072]{1,0:T(8,128)S(1)}, f32[24,3072]{1,0:T(8,128)S(1)}, u32[]{:S(2)}, u32[]{:S(2)}) collective-permute-start(f32[24,3072]{1,0:T(8,128)S(1)} %get-tuple-element.191), channel_id=1, source_target_pairs={{0,7},{1,6},{2,5},{3,4},{4,3},{5,2},{6,1},{7,0},{8,15},{9,14},{10,... | collective-permute-start | bytes 884744 | tf_op jit(solution)/shard_map/cond/branch_0_fun/ppermute | solution.py:24
  174.9 65.1 %collective-permute-start.16 = (f32[24,3072]{1,0:T(8,128)S(1)}, f32[24,3072]{1,0:T(8,128)S(1)}, u32[]{:S(2)}, u32[]{:S(2)}) collective-permute-start(f32[24,3072]{1,0:T(8,128)S(1)} %get-tuple-element.192), channel_id=1, source_target_pairs={{0,6},{1,7},{2,4},{3,5},{4,2},{5,3},{6,0},{7,1},{8,14},{9,15},{10,... | collective-permute-start | bytes 884744 | tf_op jit(solution)/shard_map/cond/branch_0_fun/ppermute | solution.py:24
  175.8 64.3 %collective-permute-start.15 = (f32[24,3072]{1,0:T(8,128)S(1)}, f32[24,3072]{1,0:T(8,128)S(1)}, u32[]{:S(2)}, u32[]{:S(2)}) collective-permute-start(f32[24,3072]{1,0:T(8,128)S(1)} %get-tuple-element.193), channel_id=1, source_target_pairs={{0,5},{1,4},{2,7},{3,6},{4,1},{5,0},{6,3},{7,2},{8,13},{9,12},{10,... | collective-permute-start | bytes 884744 | tf_op jit(solution)/shard_map/cond/branch_0_fun/ppermute | solution.py:24
  177.0 46.0 %collective-permute-start.11 = (f32[24,3072]{1,0:T(8,128)S(1)}, f32[24,3072]{1,0:T(8,128)S(1)}, u32[]{:S(2)}, u32[]{:S(2)}) collective-permute-start(f32[24,3072]{1,0:T(8,128)S(1)} %get-tuple-element.197), channel_id=1, source_target_pairs={{0,1},{1,0},{2,3},{3,2},{4,5},{5,4},{6,7},{7,6},{8,9},{9,8},{10,11... | collective-permute-start | bytes 884744 | tf_op jit(solution)/shard_map/cond/branch_0_fun/ppermute | solution.py:24
  190.6 16.7 %collective-permute-start.19 = (f32[3072]{0:T(1024)S(1)}, f32[3072]{0:T(1024)S(1)}, u32[]{:S(2)}, u32[]{:S(2)}) collective-permute-start(f32[3072]{0:T(1024)S(1)} %add.239), channel_id=1, source_target_pairs={{0,2},{1,3},{2,0},{3,1},{4,6},{5,7},{6,4},{7,5},{8,10},{9,11},{10,... | collective-permute-start | bytes 36872 | tf_op jit(solution)/shard_map/cond/branch_0_fun/ppermute | solution.py:24
  207.4 13.9 %collective-permute-start.20 = (f32[3072]{0:T(1024)S(1)}, f32[3072]{0:T(1024)S(1)}, u32[]{:S(2)}, u32[]{:S(2)}) collective-permute-start(f32[3072]{0:T(1024)S(1)} %add.240), channel_id=1, source_target_pairs={{0,4},{1,5},{2,6},{3,7},{4,0},{5,1},{6,2},{7,3},{8,12},{9,13},{10,... | collective-permute-start | bytes 36872 | tf_op jit(solution)/shard_map/cond/branch_0_fun/ppermute | solution.py:24
  221.2 18.7 %collective-permute-start.14 = (f32[24,3072]{1,0:T(8,128)S(1)}, f32[24,3072]{1,0:T(8,128)S(1)}, u32[]{:S(2)}, u32[]{:S(2)}) collective-permute-start(f32[24,3072]{1,0:T(8,128)S(1)} %get-tuple-element.194), channel_id=1, source_target_pairs={{0,4},{1,5},{2,6},{3,7},{4,0},{5,1},{6,2},{7,3},{8,12},{9,13},{10,... | collective-permute-start | bytes 884744 | tf_op jit(solution)/shard_map/cond/branch_0_fun/ppermute | solution.py:24
  223.0 8.6 %collective-permute-start.12 = (f32[24,3072]{1,0:T(8,128)S(1)}, f32[24,3072]{1,0:T(8,128)S(1)}, u32[]{:S(2)}, u32[]{:S(2)}) collective-permute-start(f32[24,3072]{1,0:T(8,128)S(1)} %get-tuple-element.196), channel_id=1, source_target_pairs={{0,2},{1,3},{2,0},{3,1},{4,6},{5,7},{6,4},{7,5},{8,10},{9,11},{10,... | collective-permute-start | bytes 884744 | tf_op jit(solution)/shard_map/cond/branch_0_fun/ppermute | solution.py:24
  231.6 8.4 %collective-permute-start.13 = (f32[24,3072]{1,0:T(8,128)S(1)}, f32[24,3072]{1,0:T(8,128)S(1)}, u32[]{:S(2)}, u32[]{:S(2)}) collective-permute-start(f32[24,3072]{1,0:T(8,128)S(1)} %get-tuple-element.195), channel_id=1, source_target_pairs={{0,3},{1,2},{2,1},{3,0},{4,7},{5,6},{6,5},{7,4},{8,11},{9,10},{10,... | collective-permute-start | bytes 884744 | tf_op jit(solution)/shard_map/cond/branch_0_fun/ppermute | solution.py:24
  (10 other events, 188.6 us)
